TPU v7x, 32 devices: a whole 2x2x4 slice. The times are simulated.
32 devices in a mesh: dp: 4 (over x, core), expert: 8 (over z, y).
Axes of the slice: x: 2, y: 2, z: 4, core: 2. Of those that a mesh axis runs over, the one named last changes fastest.
Arguments:
- tokens: bfloat16 [128, 256, 1280], P(('dp', 'expert')), may hold values from -32 to 32
- slot_keys: bfloat16 [1280, 8], replicated, may hold values from -20 to 20
- logit_scale: float32 [1], replicated, may hold values from 8 to 16
- up_weight: bfloat16 [8, 1280, 5120], P('expert', None, 'dp'), may hold values from -0.15625 to 0.15625
- up_bias: bfloat16 [8, 5120], P('expert', 'dp'), may hold values from -3 to 3
- down_weight: bfloat16 [8, 5120, 1280], P('expert', 'dp'), may hold values from -0.078125 to 0.078125
- down_bias: bfloat16 [8, 1280], replicated, may hold values from -3 to 3
Outputs:
- mixed_out: bfloat16 [128, 256, 1280], P(('dp', 'expert'))
All inputs are finite; a program needn't handle non-finite values.
Results may differ from a plain program's by a relative error of at most 0.017.
Values may be sent and summed in bfloat16 or wider, within the bound.
A program may use at most 64 MiB of HBM per device.

v0:
```python
import jax
import jax.numpy as jnp
from jax import lax
from jax.sharding import PartitionSpec as P

norm_eps = 1e-06


def unit_rms(values, axis_pos):
    return values * lax.rsqrt(jnp.mean(values * values, axis=axis_pos, keepdims=True) + norm_eps)


def body(tokens, slot_keys, logit_scale, up_weight, up_bias, down_weight, down_bias):
    images = tokens.shape[0]
    patches = tokens.shape[1]
    width = tokens.shape[2]
    per_owner = up_weight.shape[0]
    owners = lax.axis_size("expert")
    normed_tok = unit_rms(tokens.astype(jnp.float32), 2).astype(jnp.bfloat16)
    normed_keys = unit_rms(slot_keys.astype(jnp.float32), 0).astype(jnp.bfloat16)
    raw_scores = jnp.einsum(
        "ipd,dn->inp", normed_tok, normed_keys, preferred_element_type=jnp.float32
    )
    logits = logit_scale[0] * raw_scores / width
    dispatch = jax.nn.softmax(logits, axis=2).astype(jnp.bfloat16)
    combine = jax.nn.softmax(logits, axis=1).astype(jnp.bfloat16)
    slot_inputs = jnp.einsum(
        "inp,ipd->ind", dispatch, tokens, preferred_element_type=jnp.float32
    ).astype(jnp.bfloat16)
    routed = lax.all_to_all(slot_inputs, "expert", split_axis=1, concat_axis=0, tiled=True)
    pre = jnp.einsum(
        "rkd,kdf->rkf",
        lax.all_gather(routed, "dp", axis=0, tiled=True),
        up_weight,
        preferred_element_type=jnp.float32,
    )
    pre = pre + up_bias.astype(jnp.float32)[None]
    hidden = jax.nn.gelu(pre, approximate=False).astype(jnp.bfloat16)
    summed = lax.psum_scatter(
        jnp.einsum("rkf,kfd->rkd", hidden, down_weight, preferred_element_type=jnp.float32).astype(
            jnp.bfloat16
        ),
        "dp",
        scatter_dimension=0,
        tiled=True,
    ).astype(jnp.float32)
    own_bias = lax.dynamic_slice_in_dim(
        down_bias, lax.axis_index("expert") * per_owner, per_owner, 0
    ).astype(jnp.float32)
    finished = (
        (summed + own_bias[None]).astype(jnp.bfloat16).reshape(owners, images, per_owner, width)
    )
    returned = lax.all_to_all(finished, "expert", split_axis=0, concat_axis=0, tiled=True)
    weights = combine.reshape(images, owners, per_owner, patches)
    mixed_out = jnp.einsum("iekp,eikd->ipd", weights, returned, preferred_element_type=jnp.float32)
    return mixed_out.astype(jnp.bfloat16)


def solution(mesh):
    return jax.shard_map(
        body,
        mesh=mesh,
        in_specs=(
            P(("dp", "expert"), None, None),
            P(),
            P(),
            P("expert", None, "dp"),
            P("expert", "dp"),
            P("expert", "dp", None),
            P(),
        ),
        out_specs=P(("dp", "expert"), None, None),
        check_vma=False,
    )
```

profile of v0, /device:TPU:0, one launch (start us, length us, event | category | flops | bytes accessed | tf_op | source)
XLA Modules:
  0.0 83.9 jit_solution(10107239753829949492)
XLA Ops:
  6.5 0.0 copy-start
  7.3 1.0 %fusion.96 = f32[8]{0:T(128)S(1)} fusion(bf16[1280,8]{0,1:T(8,128)(2,1)} %param.8), kind=kLoop, calls=%fused_computation.87 | loop fusion | flops 30712 | bytes 20512 | tf_op jit(solution)/shard_map/reduce_sum | solution.py:10
  8.4 2.3 %fusion.2 = f32[4,256]{1,0:T(4,128)S(1)} fusion(bf16[4,256,1280]{2,1,0:T(8,128)(2,1)} %param.7), kind=kLoop, calls=%fused_computation.4 | loop fusion | flops 3931136 | bytes 2625536 | tf_op jit(solution)/shard_map/reduce_sum | solution.py:10
  10.7 0.0 copy-start.1
  10.7 2.6 %fusion.33 = f32[4,8,256]{2,1,0:T(8,128)S(1)} fusion(bf16[4,256,1280]{2,1,0:T(8,128)(2,1)} %param.7, f32[4,256]{1,0:T(4,128)S(1)} %add_rsqrt_fusion, bf16[1280,8]{0,1:T(8,128)(2,1)} %param.8, f32[8]{0:T(128)S(1)} %add_rsqrt_fusion.1, f32[]{:T(128)} %bitcast.139), kind=kOutput, calls=%fused_computation.24 | convolution fusion | flops 24950784 | bytes 2678820 | tf_op jit(solution)/shard_map/ipd,dn->inp/dot_general | solution.py:21
  13.3 0.2 fusion.133
  13.5 2.2 %convolution_convert_fusion.1 = bf16[4,8,1280]{2,1,0:T(8,128)(2,1)S(1)} fusion(bf16[4,256,1280]{2,1,0:T(8,128)(2,1)} %param.7, f32[4,8]{1,0:T(4,128)S(1)} %fusion.133, f32[4,8,256]{2,1,0:T(8,128)S(1)} %fusion.33), kind=kOutput, calls=%fused_computation.17 | convolution fusion | flops 21037344 | bytes 2736256 | tf_op jit(solution)/shard_map/inp,ipd->ind/dot_general | solution.py:27
  15.8 0.7 copy.11
  16.4 7.3 %all-to-all-start = ((bf16[4,8,1280]{2,0,1:T(4,128)(2,1)}), bf16[4,8,1280]{2,0,1:T(4,128)(2,1)S(1)}, u32[]{:S(2)}, u32[]{:S(2)}) async-start(bf16[4,8,1280]{2,0,1:T(4,128)(2,1)} %copy.11), calls=%async_computation | async-start | bytes 163840 | tf_op jit(solution)/shard_map/all_to_all | solution.py:30
  23.7 0.0 reduce-scatter.2.cloned.1.call-start
  23.8 0.0 copy-done.1
  23.8 6.9 %all-to-all-done = bf16[4,8,1280]{2,0,1:T(4,128)(2,1)S(1)} async-done(((bf16[4,8,1280]{2,0,1:T(4,128)(2,1)}), bf16[4,8,1280]{2,0,1:T(4,128)(2,1)S(1)}, u32[]{:S(2)}, u32[]{:S(2)}) %all-to-all-start) | async-done | bytes 81952 | tf_op jit(solution)/shard_map/all_to_all | solution.py:30
  30.8 6.6 %all_gather.3 = bf16[128,1,1280]{2,0,1:T(8,128)(2,1)} all-gather(bf16[32,1,1280]{2,0,1:T(8,128)(2,1)S(1)} %all_to_all.19), channel_id=1, replica_groups=mesh['dp'=4,'expert'=8] {'dp'}, dimensions={0}, use_global_device_ids=true | all-gather | bytes 409600 | tf_op jit(solution)/shard_map/all_gather | solution.py:33
  37.3 0.0 copy-done
  37.3 5.2 %fusion.20 = bf16[128,1,1280]{2,0,1:T(8,128)(2,1)} fusion(bf16[1,1280,1280]{2,1,0:T(8,128)(2,1)S(1)} %copy-done, bf16[1,1280,1280]{2,1,0:T(8,128)(2,1)} %param.10, bf16[128,1,1280]{2,0,1:T(8,128)(2,1)} %all_gather.3, f32[1280]{0:T(1024)S(1)} %convert_reduce_fusion.1), kind=kOutput, calls=%fused_computation.16 | convolution fusion | flops 849838080 | bytes 7214080 | tf_op jit(solution)/shard_map/rkf,kfd->rkd/dot_general | solution.py:40
  42.6 0.0 reduce-scatter.2.cloned.1.call-update
  42.6 0.8 convert_reduce_fusion
  43.3 17.3 %reduce-scatter.2.cloned.1.call-done = bf16[32,1,1280]{2,0,1:T(8,128)(2,1)} async-done(((bf16[128,1,1280]{2,0,1:T(8,128)(2,1)}), bf16[32,1,1280]{2,0,1:T(8,128)(2,1)}) %reduce-scatter.2.cloned.1.call-update) | async-done | bytes 81936 | tf_op jit(solution)/shard_map/reduce_scatter | solution.py:39
  60.6 0.9 %add_convert_fusion = bf16[32,1,1280]{2,0,1:T(8,128)(2,1)S(1)} fusion(bf16[32,1,1280]{2,0,1:T(8,128)(2,1)} %reduce-scatter.2.cloned.1.call-done, f32[1280]{0:T(1024)S(1)} %convert_reduce_fusion), kind=kLoop, calls=%fused_computation.82 | loop fusion | flops 122880 | bytes 168960 | tf_op jit(solution)/shard_map/convert_element_type | solution.py:51
  61.5 0.7 reshape.56
  62.2 5.5 %all-to-all-start.1 = ((bf16[8,4,1,1280]{3,1,2,0:T(4,128)(2,1)}), bf16[8,4,1,1280]{3,1,2,0:T(4,128)(2,1)S(1)}, u32[]{:S(2)}, u32[]{:S(2)}) async-start(bf16[8,4,1,1280]{3,1,2,0:T(4,128)(2,1)} %bitcast.16), calls=%async_computation.2 | async-start | bytes 163840 | tf_op jit(solution)/shard_map/all_to_all | solution.py:53
  67.7 7.0 %all-to-all-done.1 = bf16[8,4,1,1280]{3,1,2,0:T(4,128)(2,1)S(1)} async-done(((bf16[8,4,1,1280]{3,1,2,0:T(4,128)(2,1)}), bf16[8,4,1,1280]{3,1,2,0:T(4,128)(2,1)S(1)}, u32[]{:S(2)}, u32[]{:S(2)}) %all-to-all-start.1) | async-done | bytes 81952 | tf_op jit(solution)/shard_map/all_to_all | solution.py:53
  74.7 2.4 %convolution_convert_fusion = bf16[4,256,1280]{2,1,0:T(8,128)(2,1)} fusion(bf16[8,4,1,1280]{3,1,2,0:T(4,128)(2,1)S(1)} %all-to-all-done.1, f32[4,256]{1,0:T(4,128)S(1)} %fusion.134, f32[4,8,256]{2,1,0:T(8,128)S(1)} %fusion.33), kind=kOutput, calls=%fused_computation.6 | convolution fusion | flops 22307848 | bytes 2740224 | tf_op jit(solution)/shard_map/iekp,eikd->ipd/dot_general | solution.py:55
  (5 shorter events, 0.1 us)
Async XLA Ops:
  6.5 30.8 %copy-start = (bf16[1,1280,1280]{2,1,0:T(8,128)(2,1)S(1)}, bf16[1,1280,1280]{2,1,0:T(8,128)(2,1)}, u32[]{:S(2)}) copy-start(bf16[1,1280,1280]{2,1,0:T(8,128)(2,1)} %param.12) | copy-start | bytes 9830404
  10.7 13.1 %copy-start.1 = (bf16[1,1280]{1,0:T(2,128)(2,1)S(1)}, bf16[1,1280]{1,0:T(2,128)(2,1)}, u32[]{:S(2)}) copy-start(bf16[1,1280]{1,0:T(2,128)(2,1)} %param.11) | copy-start | bytes 7684
  16.4 14.3 %all-to-all-start = ((bf16[4,8,1280]{2,0,1:T(4,128)(2,1)}), bf16[4,8,1280]{2,0,1:T(4,128)(2,1)S(1)}, u32[]{:S(2)}, u32[]{:S(2)}) async-start(bf16[4,8,1280]{2,0,1:T(4,128)(2,1)} %copy.11), calls=%async_computation | async-start | bytes 163840 | tf_op jit(solution)/shard_map/all_to_all | solution.py:30
  23.7 36.9 %reduce-scatter.2.cloned.1.call-start = ((), (), s32[]{:S(2)}) async-start(), calls=%async_computation.3 | async-start | bytes 409600 | tf_op jit(solution)/shard_map/reduce_scatter | solution.py:39
  62.2 12.5 %all-to-all-start.1 = ((bf16[8,4,1,1280]{3,1,2,0:T(4,128)(2,1)}), bf16[8,4,1,1280]{3,1,2,0:T(4,128)(2,1)S(1)}, u32[]{:S(2)}, u32[]{:S(2)}) async-start(bf16[8,4,1,1280]{3,1,2,0:T(4,128)(2,1)} %bitcast.16), calls=%async_computation.2 | async-start | bytes 163840 | tf_op jit(solution)/shard_map/all_to_all | solution.py:53
Sparse Core Ops, SparseCore 0:
  42.7 17.8 reduce-scatter.1
where the time goes:
time: 84.4 us; the launch traced here: 83.9 us
  waiting for transfers between devices  31.2 us (37%)
  between operations  14.2 us (17%)
  starting transfers between devices  12.8 us (15%)
  matrix products  12.5 us (15%)
  blocking collectives  6.55 us (8%)
  other arithmetic  5.26 us (6%)
  local copies, waits for them, and re-layouts  1.37 us (2%)
    reduce_scatter x1, waiting for transfers between devices, body(): lax.psum_scatter(jnp.einsum('rkf,kfd->rkd', hidden, down_weight, preferre...  17.3 us
    all_to_all x1, starting transfers between devices, body(): lax.all_to_all(slot_inputs, 'expert', split_axis=1, concat_axis=0, tiled=...  7.31 us
    all_to_all x1, waiting for transfers between devices, body(): lax.all_to_all(finished, 'expert', split_axis=0, concat_axis=0, tiled=True)  6.98 us
    all_to_all x1, waiting for transfers between devices, body(): lax.all_to_all(slot_inputs, 'expert', split_axis=1, concat_axis=0, tiled=...  6.93 us
    all_gather x1, blocking collectives, body(): lax.all_gather(routed, 'dp', axis=0, tiled=True)  6.55 us
    all_to_all x1, starting transfers between devices, body(): lax.all_to_all(finished, 'expert', split_axis=0, concat_axis=0, tiled=True)  5.5 us
    dot_general x1, matrix products, body(): jnp.einsum('rkf,kfd->rkd', hidden, down_weight, preferred_element_type=jn...  5.22 us
    reduce_sum x2, other arithmetic, unit_rms(): jnp.mean(values * values, axis=axis_pos, keepdims=True) + norm_eps  3.35 us
  transfers between devices with their start and end apart: 3, of which 3 were waited for; matrix products, arithmetic and copies ran while one was open for 1% of the time, Pallas kernels for 0%

commit v1 on v0

--- a/solution.py
+++ b/solution.py
@@ -4,6 +4,13 @@
 from jax.sharding import PartitionSpec as P
 
 norm_eps = 1e-06
+
+
+def swap_blocks(x, axis, split, join):
+    size = lax.axis_size(axis)
+    parts = jnp.stack(jnp.split(x, size, axis=split), axis=0)
+    parts = lax.all_to_all(parts, axis, split_axis=0, concat_axis=0)
+    return jnp.concatenate(parts, axis=join)
 
 
 def unit_rms(values, axis_pos):
@@ -27,7 +34,7 @@
     slot_inputs = jnp.einsum(
         "inp,ipd->ind", dispatch, tokens, preferred_element_type=jnp.float32
     ).astype(jnp.bfloat16)
-    routed = lax.all_to_all(slot_inputs, "expert", split_axis=1, concat_axis=0, tiled=True)
+    routed = swap_blocks(slot_inputs, "expert", 1, 0)
     pre = jnp.einsum(
         "rkd,kdf->rkf",
         lax.all_gather(routed, "dp", axis=0, tiled=True),

time: 84.4 us -> 88.7 us (1.051)
  local copies, waits for them, and re-layouts: 1.37 us -> 5.67 us
    unnamed x4 -> x11, local copies, waits for them, and re-layouts: 0.01 us -> 4.24 us
where the time goes in v1:
time: 88.7 us; the launch traced here: 88.2 us
  waiting for transfers between devices  31.2 us (35%)
  between operations  14.3 us (16%)
  starting transfers between devices  12.8 us (14%)
  matrix products  12.5 us (14%)
  blocking collectives  6.55 us (7%)
  local copies, waits for them, and re-layouts  5.67 us (6%)
  other arithmetic  5.26 us (6%)
    reduce_scatter x1, waiting for transfers between devices, body(): lax.psum_scatter(jnp.einsum('rkf,kfd->rkd', hidden, down_weight, preferre...  17.3 us
    all_to_all x1, starting transfers between devices, swap_blocks(): parts = lax.all_to_all(parts, axis, split_axis=0, concat_axis=0)  7.31 us
    all_to_all x1, waiting for transfers between devices, body(): lax.all_to_all(finished, 'expert', split_axis=0, concat_axis=0, tiled=True)  6.98 us
    all_to_all x1, waiting for transfers between devices, swap_blocks(): parts = lax.all_to_all(parts, axis, split_axis=0, concat_axis=0)  6.93 us
    all_gather x1, blocking collectives, body(): lax.all_gather(routed, 'dp', axis=0, tiled=True)  6.55 us
    all_to_all x1, starting transfers between devices, body(): lax.all_to_all(finished, 'expert', split_axis=0, concat_axis=0, tiled=True)  5.5 us
    dot_general x1, matrix products, body(): jnp.einsum('rkf,kfd->rkd', hidden, down_weight, preferred_element_type=jn...  5.22 us
    unnamed x11, local copies, waits for them, and re-layouts  4.24 us
  transfers between devices with their start and end apart: 3, of which 3 were waited for; matrix products, arithmetic and copies ran while one was open for 1% of the time, Pallas kernels for 0%

profile of v1, /device:TPU:0, one launch (start us, length us, event | category | flops | bytes accessed | tf_op | source)
XLA Modules:
  0.0 88.2 jit_solution(1371782699578867841)
XLA Ops:
  6.5 0.0 copy-start
  7.3 1.0 %fusion.96 = f32[8]{0:T(128)S(1)} fusion(bf16[1280,8]{0,1:T(8,128)(2,1)} %param.8), kind=kLoop, calls=%fused_computation.87 | loop fusion | flops 30712 | bytes 20512 | tf_op jit(solution)/shard_map/reduce_sum | solution.py:17
  8.4 2.3 %fusion.2 = f32[4,256]{1,0:T(4,128)S(1)} fusion(bf16[4,256,1280]{2,1,0:T(8,128)(2,1)} %param.7), kind=kLoop, calls=%fused_computation.4 | loop fusion | flops 3931136 | bytes 2625536 | tf_op jit(solution)/shard_map/reduce_sum | solution.py:17
  10.7 0.0 copy-start.1
  10.7 2.6 %fusion.33 = f32[4,8,256]{2,1,0:T(8,128)S(1)} fusion(bf16[4,256,1280]{2,1,0:T(8,128)(2,1)} %param.7, f32[4,256]{1,0:T(4,128)S(1)} %add_rsqrt_fusion, bf16[1280,8]{0,1:T(8,128)(2,1)} %param.8, f32[8]{0:T(128)S(1)} %add_rsqrt_fusion.1, f32[]{:T(128)} %bitcast.152), kind=kOutput, calls=%fused_computation.24 | convolution fusion | flops 24950784 | bytes 2678820 | tf_op jit(solution)/shard_map/ipd,dn->inp/dot_general | solution.py:28
  13.3 0.2 fusion.134
  13.5 2.2 %convolution_convert_fusion.1 = bf16[4,8,1280]{2,1,0:T(8,128)(2,1)S(1)} fusion(bf16[4,256,1280]{2,1,0:T(8,128)(2,1)} %param.7, f32[4,8]{1,0:T(4,128)S(1)} %fusion.134, f32[4,8,256]{2,1,0:T(8,128)S(1)} %fusion.33), kind=kOutput, calls=%fused_computation.17 | convolution fusion | flops 21037344 | bytes 2736256 | tf_op jit(solution)/shard_map/inp,ipd->ind/dot_general | solution.py:34
  15.8 0.1 fusion.133
  15.9 0.6 constant_dynamic-update-slice_fusion.7
  16.5 0.6 constant_dynamic-update-slice_fusion.6
  17.1 0.6 constant_dynamic-update-slice_fusion.5
  17.7 0.6 constant_dynamic-update-slice_fusion.4
  18.3 0.6 constant_dynamic-update-slice_fusion.3
  18.9 0.6 constant_dynamic-update-slice_fusion.2
  19.5 0.6 constant_dynamic-update-slice_fusion.1
  20.1 0.6 constant_dynamic-update-slice_fusion
  20.8 7.3 %all-to-all-start = ((bf16[8,4,1,1280]{3,1,2,0:T(4,128)(2,1)}), bf16[8,4,1,1280]{3,1,2,0:T(4,128)(2,1)S(1)}, u32[]{:S(2)}, u32[]{:S(2)}) async-start(bf16[8,4,1,1280]{3,1,2,0:T(4,128)(2,1)} %constant_dynamic-update-slice_fusion), calls=%async_computation | async-start | bytes 163840 | tf_op jit(solution)/shard_map/all_to_all | solution.py:12
  28.1 0.0 reduce-scatter.2.cloned.1.call-start
  28.1 0.0 copy-done.1
  28.1 6.9 %all-to-all-done = bf16[8,4,1,1280]{3,1,2,0:T(4,128)(2,1)S(1)} async-done(((bf16[8,4,1,1280]{3,1,2,0:T(4,128)(2,1)}), bf16[8,4,1,1280]{3,1,2,0:T(4,128)(2,1)S(1)}, u32[]{:S(2)}, u32[]{:S(2)}) %all-to-all-start) | async-done | bytes 81952 | tf_op jit(solution)/shard_map/all_to_all | solution.py:12
  35.1 6.6 %all_gather.3 = bf16[128,1,1280]{2,0,1:T(8,128)(2,1)} all-gather(bf16[32,1,1280]{2,0,1:T(8,128)(2,1)S(1)} %reshape.55), channel_id=1, replica_groups=mesh['dp'=4,'expert'=8] {'dp'}, dimensions={0}, use_global_device_ids=true | all-gather | bytes 409600 | tf_op jit(solution)/shard_map/all_gather | solution.py:40
  41.7 0.0 copy-done
  41.7 5.2 %fusion.20 = bf16[128,1,1280]{2,0,1:T(8,128)(2,1)} fusion(bf16[1,1280,1280]{2,1,0:T(8,128)(2,1)S(1)} %copy-done, bf16[1,1280,1280]{2,1,0:T(8,128)(2,1)} %param.10, bf16[128,1,1280]{2,0,1:T(8,128)(2,1)} %all_gather.3, f32[1280]{0:T(1024)S(1)} %convert_reduce_fusion.1), kind=kOutput, calls=%fused_computation.16 | convolution fusion | flops 849838080 | bytes 7214080 | tf_op jit(solution)/shard_map/rkf,kfd->rkd/dot_general | solution.py:47
  46.9 0.0 reduce-scatter.2.cloned.1.call-update
  46.9 0.8 convert_reduce_fusion
  47.7 17.3 %reduce-scatter.2.cloned.1.call-done = bf16[32,1,1280]{2,0,1:T(8,128)(2,1)} async-done(((bf16[128,1,1280]{2,0,1:T(8,128)(2,1)}), bf16[32,1,1280]{2,0,1:T(8,128)(2,1)}) %reduce-scatter.2.cloned.1.call-update) | async-done | bytes 81936 | tf_op jit(solution)/shard_map/reduce_scatter | solution.py:46
  64.9 0.9 %add_convert_fusion = bf16[32,1,1280]{2,0,1:T(8,128)(2,1)S(1)} fusion(bf16[32,1,1280]{2,0,1:T(8,128)(2,1)} %reduce-scatter.2.cloned.1.call-done, f32[1280]{0:T(1024)S(1)} %convert_reduce_fusion), kind=kLoop, calls=%fused_computation.82 | loop fusion | flops 122880 | bytes 168960 | tf_op jit(solution)/shard_map/convert_element_type | solution.py:58
  65.8 0.7 reshape.60
  66.5 5.5 %all-to-all-start.1 = ((bf16[8,4,1,1280]{3,1,2,0:T(4,128)(2,1)}), bf16[8,4,1,1280]{3,1,2,0:T(4,128)(2,1)S(1)}, u32[]{:S(2)}, u32[]{:S(2)}) async-start(bf16[8,4,1,1280]{3,1,2,0:T(4,128)(2,1)} %bitcast.14), calls=%async_computation.2 | async-start | bytes 163840 | tf_op jit(solution)/shard_map/all_to_all | solution.py:60
  72.0 7.0 %all-to-all-done.1 = bf16[8,4,1,1280]{3,1,2,0:T(4,128)(2,1)S(1)} async-done(((bf16[8,4,1,1280]{3,1,2,0:T(4,128)(2,1)}), bf16[8,4,1,1280]{3,1,2,0:T(4,128)(2,1)S(1)}, u32[]{:S(2)}, u32[]{:S(2)}) %all-to-all-start.1) | async-done | bytes 81952 | tf_op jit(solution)/shard_map/all_to_all | solution.py:60
  79.0 2.4 %convolution_convert_fusion = bf16[4,256,1280]{2,1,0:T(8,128)(2,1)} fusion(bf16[8,4,1,1280]{3,1,2,0:T(4,128)(2,1)S(1)} %all-to-all-done.1, f32[4,256]{1,0:T(4,128)S(1)} %fusion.135, f32[4,8,256]{2,1,0:T(8,128)S(1)} %fusion.33), kind=kOutput, calls=%fused_computation.6 | convolution fusion | flops 22307848 | bytes 2740224 | tf_op jit(solution)/shard_map/iekp,eikd->ipd/dot_general | solution.py:62
  (5 shorter events, 0.1 us)
Async XLA Ops:
  6.5 35.1 %copy-start = (bf16[1,1280,1280]{2,1,0:T(8,128)(2,1)S(1)}, bf16[1,1280,1280]{2,1,0:T(8,128)(2,1)}, u32[]{:S(2)}) copy-start(bf16[1,1280,1280]{2,1,0:T(8,128)(2,1)} %param.12) | copy-start | bytes 9830404
  10.7 17.4 %copy-start.1 = (bf16[1,1280]{1,0:T(2,128)(2,1)S(1)}, bf16[1,1280]{1,0:T(2,128)(2,1)}, u32[]{:S(2)}) copy-start(bf16[1,1280]{1,0:T(2,128)(2,1)} %param.11) | copy-start | bytes 7684
  20.8 14.3 %all-to-all-start = ((bf16[8,4,1,1280]{3,1,2,0:T(4,128)(2,1)}), bf16[8,4,1,1280]{3,1,2,0:T(4,128)(2,1)S(1)}, u32[]{:S(2)}, u32[]{:S(2)}) async-start(bf16[8,4,1,1280]{3,1,2,0:T(4,128)(2,1)} %constant_dynamic-update-slice_fusion), calls=%async_computation | async-start | bytes 163840 | tf_op jit(solution)/shard_map/all_to_all | solution.py:12
  28.1 36.8 %reduce-scatter.2.cloned.1.call-start = ((), (), s32[]{:S(2)}) async-start(), calls=%async_computation.3 | async-start | bytes 409600 | tf_op jit(solution)/shard_map/reduce_scatter | solution.py:46
  66.5 12.5 %all-to-all-start.1 = ((bf16[8,4,1,1280]{3,1,2,0:T(4,128)(2,1)}), bf16[8,4,1,1280]{3,1,2,0:T(4,128)(2,1)S(1)}, u32[]{:S(2)}, u32[]{:S(2)}) async-start(bf16[8,4,1,1280]{3,1,2,0:T(4,128)(2,1)} %bitcast.14), calls=%async_computation.2 | async-start | bytes 163840 | tf_op jit(solution)/shard_map/all_to_all | solution.py:60
Sparse Core Ops, SparseCore 0:
  47.0 17.8 reduce-scatter.1
